TPU v7x, 32 devices: a whole 2x2x4 slice. The times are simulated.
32 devices in a mesh: blk: 8 (over y, x, core), grp: 4 (over z).
Axes of the slice: x: 2, y: 2, z: 4, core: 2. Of those that a mesh axis runs over, the one named last changes fastest.
Arguments:
- samples: float32 [32, 128, 256], P('blk', 'grp'), may hold values from -11 to 11
- pair_table: int32 [32, 16], P('blk'), may hold values from 0 to 31
- assignment: int32 [2, 32], P(None, 'blk'), may hold values from 0 to 127
- band_index: int32 [2], replicated, may hold values from 0 to 1023
Outputs:
- log_weight: float32 [2, 32, 128], P(None, 'blk', 'grp')
All inputs are finite; a program needn't handle non-finite values.
Results may differ from a plain program's by a relative error of at most 0.0003.
Values sent between devices are 32-bit elements; how exact they have to be, the bound alone decides.
No kernel may reach another device: no remote copies, remote signals or barrier semaphores. Data moves between devices by JAX's collectives and lax.ppermute only.
A program may use at most 128 MiB of HBM per device.

v0:
```python
import jax
import jax.numpy as jnp
from jax import lax
from jax.sharding import PartitionSpec as P

PAIRS = 16


def joined_2(shard, axis, combine):
    everything = jax.tree.map(lambda part: lax.all_gather(part, axis), shard)
    initial = jax.tree.map(lambda part: part[0], everything)

    def hop(k, so_far):
        return combine(so_far, jax.tree.map(lambda part: part[k], everything))

    return lax.fori_loop(1, lax.axis_size(axis), hop, initial)


def make_fold(queries, query_norm, band_list, counts):

    def fold(state, shard_rows, offset):
        count_in = shard_rows.shape[0]
        rows_dev = shard_rows.shape[1]

        def compute(inner):
            key_rows = shard_rows.reshape(count_in * rows_dev, shard_rows.shape[2])
            key_norm = jnp.sum(key_rows * key_rows, -1)
            product = jnp.einsum("qd,kd->qk", queries, key_rows, precision=lax.Precision.HIGHEST)
            distance = query_norm[:, None] + key_norm[None, :] - 2.0 * product
            blocks = []
            for band_sq in band_list:
                scores = (-distance / (2.0 * band_sq)).reshape(
                    distance.shape[0], count_in, rows_dev
                )
                peak = jnp.max(scores, -1)
                blocks.append(peak + jnp.log(jnp.sum(jnp.exp(scores - peak[..., None]), -1)))
            update = jnp.stack(blocks)
            return lax.dynamic_update_slice(inner, update, (0, 0, offset))

        needed = jnp.any(counts > 0)
        return lax.cond(needed, compute, lambda inner: inner, state)

    return fold


def per_device(samples, pair_table, assignment, band_index):
    local_subs, rows_dev, width = samples.shape
    rounds = assignment.shape[0]
    group_size = lax.axis_size("grp")
    group_index = lax.axis_index("grp")
    members = local_subs * lax.axis_size("blk")
    band_sq = width * (1.0 + band_index.astype(jnp.float32) / 256.0) / 32.0
    local_pick = assignment - group_index * rows_dev
    onehot = (
        local_pick[:, :, None] == jnp.arange(rows_dev, dtype=jnp.int32)[None, None, :]
    ).astype(jnp.float32)
    picked = jnp.einsum("tsr,srd->td", onehot, samples, precision=lax.Precision.HIGHEST)
    centre = lax.psum(picked, ("blk", "grp")) / members
    member_ids = jnp.arange(members, dtype=jnp.int32)
    count_int = jnp.sum(
        (pair_table[:, :, None] == member_ids[None, None, :]).astype(jnp.int32), axis=1
    )
    counts = count_int.astype(jnp.float32)
    gathered = lax.all_gather(samples, "grp", axis=1, tiled=True)
    query_count = local_subs * rows_dev * group_size
    queries = gathered.reshape(query_count, width)
    query_norm = jnp.sum(queries * queries, -1)
    start_state = jnp.zeros((rounds, query_count, members), jnp.float32)
    fold = make_fold(queries, query_norm, [band_sq[turn] for turn in range(rounds)], count_int)
    partial_value = fold(
        start_state, lax.all_gather(samples, "blk", axis=0, tiled=True), jnp.int32(0)
    )
    split_view = partial_value.reshape(rounds, local_subs, group_size, rows_dev, members)
    swapped = lax.all_to_all(split_view, "grp", split_axis=2, concat_axis=2, tiled=True)
    peak = jnp.max(swapped, 2)
    kernel = peak + jnp.log(jnp.sum(jnp.exp(swapped - peak[:, :, None]), 2))
    weighted = jnp.einsum("tsrm,sm->tsr", kernel, counts, precision=lax.Precision.HIGHEST) / PAIRS
    spread = samples[None] - centre[:, None, None, :]
    logits = weighted - jnp.sum(spread * spread, -1) / (2.0 * band_sq[:, None, None])
    row_peak = jnp.max(logits, -1)
    row_total = jnp.sum(jnp.exp(logits - row_peak[..., None]), -1)

    def combine_pair(first, second):
        joined = jnp.maximum(first[0], second[0])
        return (
            joined,
            first[1] * jnp.exp(first[0] - joined) + second[1] * jnp.exp(second[0] - joined),
        )

    peak_all, total_all = joined_2((row_peak, row_total), "grp", combine_pair)
    return logits - peak_all[..., None] - jnp.log(total_all)[..., None]


def solution(mesh):
    return jax.shard_map(
        per_device,
        mesh=mesh,
        in_specs=(P("blk", "grp", None), P("blk", None), P(None, "blk"), P()),
        out_specs=P(None, "blk", "grp"),
        check_vma=False,
    )
```

profile of v0, /device:TPU:0, one launch (start us, length us, event | category | flops | bytes accessed | tf_op | source)
XLA Modules:
  0.0 123.1 jit_solution(9642932200936565193)
XLA Ops:
  6.5 0.7 all-gather.6.cloned.1.call-update
  7.3 0.8 convert_reduce_fusion
  8.0 0.6 compare_reduce_fusion
  9.3 0.7 broadcast_subtract_fusion
  10.1 1.2 convolution_bitcast_fusion
  11.3 42.0 %psum.7 = f32[2,256]{1,0:T(2,128)S(1)} all-reduce(f32[2,256]{1,0:T(2,128)S(1)} %convolution_bitcast_fusion), channel_id=1, replica_groups=mesh['blk'=8,'grp'=4] {'blk','grp'}, use_global_device_ids=true, to_apply=%region_12.0 | all-reduce | flops 512 | bytes 4096 | tf_op jit(solution)/shard_map/psum | solution.py:58
  53.2 15.9 %all_gather.18 = f32[4,128,256]{2,1,0:T(8,128)S(1)} all-gather(f32[4,32,256]{2,1,0:T(8,128)} %param.8), channel_id=1, replica_groups=mesh['blk'=8,'grp'=4] {'grp'}, dimensions={1}, use_global_device_ids=true | all-gather | bytes 655360 | tf_op jit(solution)/shard_map/all_gather | solution.py:64
  69.2 0.7 multiply_add_fusion
  69.8 14.7 %conditional.1 = (f32[2,512,32]{1,2,0:T(8,128)S(1)}) conditional(s32[]{:T(128)} %convert_element_type.15, () %tuple.36, (f32[4,128,256]{2,1,0:T(8,128)S(1)}, f32[32,32,256]{2,1,0:T(8,128)}, f32[2]{0:T(128)S(1)}) %tuple.37), branch_computations={%region_2.0_spmd, %region_3.10_spmd} | conditional | flops 1617689088 | bytes 25186376 | solution.py:41
  69.8 1.4 %multiply_reduce_fusion = f32[32,32]{1,0:T(8,128)S(1)} fusion(f32[32,32,256]{2,1,0:T(8,128)} %get-tuple-element.164), kind=kLoop, calls=%fused_computation.11 | loop fusion | flops 523264 | bytes 1052672 | tf_op jit(solution)/shard_map/cond/branch_1_fun/reduce_sum | solution.py:27
  71.3 0.7 fusion.12
  73.5 5.3 %broadcast_divide_fusion.1 = (f32[512,1024]{1,0:T(8,128)}, f32[512,1024]{1,0:T(8,128)}) fusion(f32[]{:T(128)} %bitcast.3, f32[]{:T(128)} %bitcast.6, f32[512,256]{1,0:T(8,128)S(1)} %bitcast.71, f32[1024,256]{1,0:T(8,128)} %bitcast.74, f32[1024]{0:T(1024)S(1)} %add.87, f32[512]{0:T(512)S(1)} %bitcast.80), kind=kOutput, calls=%fused_computation.10 | convolution fusion | flops 1613758464 | bytes 5773320 | tf_op jit(solution)/shard_map/cond/branch_1_fun/qd,kd->qk/dot_general | solution.py:28
  78.8 1.9 %copy.16 = f32[512,1024]{0,1:T(8,128)S(1)} copy(f32[512,1024]{1,0:T(8,128)} %get-tuple-element.190) | data formatting | bytes 4194304 | tf_op jit(solution)/shard_map/cond/branch_1_fun/div | solution.py:32
  81.1 0.5 fusion.3
  81.6 1.9 %copy.17 = f32[512,1024]{0,1:T(8,128)S(1)} copy(f32[512,1024]{1,0:T(8,128)} %get-tuple-element.191) | data formatting | bytes 4194304 | tf_op jit(solution)/shard_map/cond/branch_1_fun/div | solution.py:32
  83.9 0.5 fusion.1
  84.9 1.0 reshape.97
  85.9 3.8 %all-to-all-start = ((f32[4,1,8192]{2,1,0:T(1,128)}), f32[4,1,8192]{2,1,0:T(1,128)S(1)}, u32[]{:S(2)}, u32[]{:S(2)}) async-start(f32[4,1,8192]{2,1,0:T(1,128)} %reshape.97), calls=%async_computation | async-start | bytes 262144 | tf_op jit(solution)/shard_map/all_to_all | solution.py:74
  89.8 5.8 %all-to-all-done = f32[4,1,8192]{2,1,0:T(1,128)S(1)} async-done(((f32[4,1,8192]{2,1,0:T(1,128)}), f32[4,1,8192]{2,1,0:T(1,128)S(1)}, u32[]{:S(2)}, u32[]{:S(2)}) %all-to-all-start) | async-done | bytes 131104 | tf_op jit(solution)/shard_map/all_to_all | solution.py:74
  95.6 0.5 broadcast.44
  96.1 1.0 reduce.5
  98.3 9.0 %all-gather.3 = f32[4,2,4]{2,1,0:T(2,128)S(1)} all-gather(f32[1,2,4]{2,1,0:T(2,128)S(1)} %bitcast.79), channel_id=3, replica_groups=mesh['blk'=8,'grp'=4] {'grp'}, dimensions={0}, use_global_device_ids=true | all-gather | bytes 160 | tf_op jit(solution)/shard_map/all_gather | solution.py:10
  107.3 8.2 %all-gather.2 = f32[4,2,4]{2,1,0:T(2,128)S(1)} all-gather(f32[1,2,4]{2,1,0:T(2,128)S(1)} %bitcast.77), channel_id=2, replica_groups=mesh['blk'=8,'grp'=4] {'grp'}, dimensions={0}, use_global_device_ids=true | all-gather | bytes 160 | tf_op jit(solution)/shard_map/all_gather | solution.py:10
  115.6 0.7 subtract_subtract_fusion
  (31 shorter events, 2.9 us)
Async XLA Ops:
  6.5 63.3 %all-gather.6.cloned.1.call-start = ((), (), s32[]{:S(2)}) async-start(), calls=%async_computation.1 | async-start | bytes 1179648 | tf_op jit(solution)/shard_map/all_gather | solution.py:71
  84.5 5.2 %copy-start = (f32[4,32,256]{2,1,0:T(8,128)S(1)}, f32[4,32,256]{2,1,0:T(8,128)}, u32[]{:S(2)}) copy-start(f32[4,32,256]{2,1,0:T(8,128)} %param.8) | copy-start | bytes 393220
  85.9 9.7 %all-to-all-start = ((f32[4,1,8192]{2,1,0:T(1,128)}), f32[4,1,8192]{2,1,0:T(1,128)S(1)}, u32[]{:S(2)}, u32[]{:S(2)}) async-start(f32[4,1,8192]{2,1,0:T(1,128)} %reshape.97), calls=%async_computation | async-start | bytes 262144 | tf_op jit(solution)/shard_map/all_to_all | solution.py:74
Sparse Core Ops, SparseCore 0:
  9.2 26.2 all-gather.5
where the time goes:
time: 124 us; the launch traced here: 123 us
  blocking collectives  75 us (60%)
  between operations  14.1 us (11%)
  other arithmetic  8.66 us (7%)
  local copies, waits for them, and re-layouts  6.86 us (6%)
  matrix products  6.7 us (5%)
  waiting for transfers between devices  6.5 us (5%)
  starting transfers between devices  3.8 us (3%)
  loops' own time  1.43 us (1%)
    psum x1, blocking collectives, per_device(): centre = lax.psum(picked, ('blk', 'grp')) / members  42 us
    all_gather x2, blocking collectives, joined_2(): everything = jax.tree.map(lambda part: lax.all_gather(part, axis), shard)  17.2 us
    all_gather x1, blocking collectives, per_device(): gathered = lax.all_gather(samples, 'grp', axis=1, tiled=True)  15.9 us
    all_to_all x1, waiting for transfers between devices, per_device(): lax.all_to_all(split_view, 'grp', split_axis=2, concat_axis=2, tiled=True)  5.79 us
    dot_general x1, matrix products, compute(): jnp.einsum('qd,kd->qk', queries, key_rows, precision=lax.Precision.HIGHEST)  5.35 us
    div x2, local copies, waits for them, and re-layouts, compute(): -distance / (2.0 * band_sq)  3.84 us
    all_to_all x1, starting transfers between devices, per_device(): lax.all_to_all(split_view, 'grp', split_axis=2, concat_axis=2, tiled=True)  3.8 us
  transfers between devices with their start and end apart: 2, of which 1 were waited for; matrix products, arithmetic and copies ran while one was open for 3% of the time, Pallas kernels for 0%

commit v1 on v0

v1 whole, which is shorter than its diff:
```python
import functools

import jax
import jax.numpy as jnp
from jax import lax
from jax.experimental import pallas as pl
from jax.experimental.pallas import tpu as pltpu
from jax.sharding import PartitionSpec as P

HIGH = lax.Precision.HIGHEST
NT = (((1,), (1,)), ((), ()))
NN = (((1,), (0,)), ((), ()))


def dot(a, b, dims):
    return lax.dot_general(a, b, dims, precision=HIGH, preferred_element_type=jnp.float32)


def inverse_width(band_ref, turn, width, shape):
    index = jnp.full(shape, band_ref[turn], jnp.int32).astype(jnp.float32)
    band_sq = width * (1.0 + index / 256.0) / 32.0
    return 1.0 / (2.0 * band_sq)


def prepare_kernel(group_ref, assign_ref, x_ref, out_ref, *, subs, rows, rounds):
    first = group_ref[0] * rows
    lane = lax.broadcasted_iota(jnp.int32, (8, subs * rows), 1)
    line = lax.broadcasted_iota(jnp.int32, (8, subs * rows), 0)
    weight = jnp.zeros((8, subs * rows), jnp.float32)
    for turn in range(rounds):
        for sub in range(subs):
            local = assign_ref[turn, sub] - first
            inside = jnp.logical_and(local >= 0, local < rows)
            target = jnp.where(inside, sub * rows + local, -1)
            weight = jnp.where(
                jnp.logical_and(line == turn, lane == target), 1.0, weight
            )
    x = x_ref[...]
    out_ref[: subs * rows, :] = x
    out_ref[subs * rows :, :] = dot(weight, x, NN)


def score_kernel(
    band_ref, hot_ref, *refs, blocks, groups, subs, rows, rounds, pairs, members
):
    key_refs = refs[:blocks]
    query_refs = refs[blocks : blocks + groups - 1]
    out_ref, norm_ref, queries, low, totals = refs[blocks + groups - 1 :]
    lanes = subs * rows
    width = queries.shape[1]
    count = groups * lanes
    queries[:lanes, :] = key_refs[0][:lanes, :]
    for k in range(1, groups):
        queries[k * lanes : (k + 1) * lanes, :] = query_refs[k - 1][...]
    q = queries[...]
    query_norm = dot(jnp.ones((8, width), jnp.float32), q * q, NT)[:1]
    inverse = [inverse_width(band_ref, turn, width, (1, count)) for turn in range(rounds)]
    q2 = -2.0 * q
    centre = jnp.zeros((8, width), jnp.float32)
    for block in range(blocks):
        keys = key_refs[block][:lanes, :]
        centre += key_refs[block][lanes:, :]
        key_norm = jnp.sum(keys * keys, -1, keepdims=True)
        part = (key_norm + dot(keys, q2, NT)).reshape(subs, rows, count)
        smallest = jnp.min(part, 1)
        gap = smallest[:, None, :] - part
        here = slice(block * subs, (block + 1) * subs)
        low[here, :] = smallest
        for turn in range(rounds):
            totals[turn, here, :] = jnp.sum(jnp.exp(gap * inverse[turn][:, None, :]), 1)
    centre = centre / members
    cross = dot(centre, q, NT)
    nearest = low[...] + query_norm
    hot = hot_ref[...]
    lane = lax.broadcasted_iota(jnp.int32, (pairs, lanes), 1) // rows
    for turn in range(rounds):
        value = jnp.log(totals[turn]) - nearest * inverse[turn]
        chosen = dot(hot, value, NN)
        for k in range(groups):
            piece = chosen[:, k * lanes : (k + 1) * lanes]
            merged = piece[:pairs]
            for sub in range(1, subs):
                merged = jnp.where(lane == sub, piece[sub * pairs : (sub + 1) * pairs], merged)
            at = (k * rounds + turn) * pairs
            out_ref[at : at + pairs, :] = merged
    base = groups * rounds * pairs
    for k in range(groups):
        out_ref[base + k * rounds : base + (k + 1) * rounds, :] = cross[
            :rounds, k * lanes : (k + 1) * lanes
        ]
        norm_ref[k : k + 1, :] = query_norm[:, k * lanes : (k + 1) * lanes]
    base += groups * rounds
    for c in range(width // lanes):
        out_ref[base + c * 8 : base + (c + 1) * 8, :] = centre[:, c * lanes : (c + 1) * lanes]


def finish_kernel(band_ref, norm_ref, *refs, groups, subs, rows, rounds, pairs, width):
    parts = refs[:groups]
    out_ref = refs[groups]
    lanes = subs * rows
    base = groups * rounds * pairs
    tail = base + groups * rounds
    centre = [
        sum(part[tail + c * 8 : tail + (c + 1) * 8, :] for part in parts)
        for c in range(width // lanes)
    ]
    centre_sq = sum(jnp.sum(c * c, -1, keepdims=True) for c in centre)
    group_of = lax.broadcasted_iota(jnp.int32, (1, lanes), 1) // rows
    for turn in range(rounds):
        inverse = inverse_width(band_ref, turn, width, (1, lanes))
        logits = []
        for k in range(groups):
            pieces = []
            cross = jnp.zeros((1, lanes), jnp.float32)
            for j in range(groups):
                at = ((k ^ j) * rounds + turn) * pairs
                pieces.append(parts[j][at : at + pairs, :])
                row = base + (k ^ j) * rounds + turn
                cross = cross + parts[j][row : row + 1, :]
            peak = functools.reduce(jnp.maximum, pieces)
            total = sum(jnp.exp(piece - peak) for piece in pieces)
            kernel = peak + jnp.log(total)
            weighted = jnp.sum(kernel, 0, keepdims=True) / pairs
            spread = norm_ref[k : k + 1, :] - 2.0 * cross + centre_sq[turn : turn + 1, :]
            logits.append(weighted - spread * inverse)
        peak = functools.reduce(jnp.maximum, logits)
        row_peak = jnp.zeros((1, lanes), jnp.float32)
        for sub in range(subs):
            here = jnp.max(jnp.where(group_of == sub, peak, -jnp.inf), -1, keepdims=True)
            row_peak = jnp.where(group_of == sub, here, row_peak)
        total = sum(jnp.exp(value - row_peak) for value in logits)
        for sub in range(subs):
            here = jnp.sum(jnp.where(group_of == sub, total, 0.0), -1, keepdims=True)
            value = logits[0] - row_peak - jnp.log(here)
            out_ref[turn, sub : sub + 1, :] = value[:, sub * rows : (sub + 1) * rows]


def per_device(samples, pair_table, assignment, band_index):
    subs, rows, width = samples.shape
    rounds = assignment.shape[0]
    pairs = pair_table.shape[1]
    groups = lax.axis_size("grp")
    blocks = lax.axis_size("blk")
    members = subs * blocks
    lanes = subs * rows
    group = lax.axis_index("grp")
    block = lax.axis_index("blk")

    def over(axis, size, value, k):
        return lax.ppermute(value, axis, [(i, i ^ k) for i in range(size)])

    smem = pl.BlockSpec(memory_space=pltpu.SMEM)
    vmem = pl.BlockSpec(memory_space=pltpu.VMEM)
    x = samples.reshape(lanes, width)
    queries = [over("grp", groups, x, k) for k in range(1, groups)]
    own = pl.pallas_call(
        functools.partial(prepare_kernel, subs=subs, rows=rows, rounds=rounds),
        out_shape=jax.ShapeDtypeStruct((lanes + 8, width), jnp.float32),
        in_specs=[smem, smem, vmem],
        out_specs=vmem,
        name="prepare",
    )(group[None], assignment, x)
    keys = {0: own}
    for k in range(2, blocks, 2):
        keys[k] = over("blk", blocks, own, k)
    for k in range(0, blocks, 2):
        keys[k ^ 1] = over("blk", blocks, keys[k], 1)
    place = (pair_table // subs ^ block) * subs + pair_table % subs
    hot = (
        place.reshape(subs * pairs, 1) == jnp.arange(members, dtype=jnp.int32)[None, :]
    ).astype(jnp.float32)
    height = groups * rounds * pairs + groups * rounds + 8 * (width // lanes)
    part, norm = pl.pallas_call(
        functools.partial(
            score_kernel,
            blocks=blocks,
            groups=groups,
            subs=subs,
            rows=rows,
            rounds=rounds,
            pairs=pairs,
            members=members,
        ),
        out_shape=(
            jax.ShapeDtypeStruct((height, lanes), jnp.float32),
            jax.ShapeDtypeStruct((groups, lanes), jnp.float32),
        ),
        in_specs=[smem] + [vmem] * (blocks + groups),
        out_specs=(vmem, vmem),
        scratch_shapes=[
            pltpu.VMEM((groups * lanes, width), jnp.float32),
            pltpu.VMEM((members, groups * lanes), jnp.float32),
            pltpu.VMEM((rounds, members, groups * lanes), jnp.float32),
        ],
        name="score",
    )(band_index, hot, *[keys[k] for k in range(blocks)], *queries)
    parts = [part] + [over("grp", groups, part, k) for k in range(1, groups)]
    return pl.pallas_call(
        functools.partial(
            finish_kernel,
            groups=groups,
            subs=subs,
            rows=rows,
            rounds=rounds,
            pairs=pairs,
            width=width,
        ),
        out_shape=jax.ShapeDtypeStruct((rounds, subs, rows), jnp.float32),
        in_specs=[smem] + [vmem] * (groups + 1),
        out_specs=vmem,
        name="finish",
    )(band_index, norm, *parts)


def solution(mesh):
    return jax.shard_map(
        per_device,
        mesh=mesh,
        in_specs=(P("blk", "grp", None), P("blk", None), P(None, "blk"), P()),
        out_specs=P(None, "blk", "grp"),
        check_vma=False,
    )
```

time: 124 us -> 41.1 us (0.33)
  blocking collectives: 75 us -> 0 us
  starting transfers between devices: 3.8 us -> 17.8 us
  between operations: 14.1 us -> 0.12 us
  Pallas kernels: 0 us -> 11.5 us
  other arithmetic: 8.66 us -> 0.7 us
  matrix products: 6.7 us -> 0 us
  local copies, waits for them, and re-layouts: 6.86 us -> 2.83 us
  loops' own time: 1.43 us -> 0 us
  waiting for transfers between devices: 6.5 us -> 7.92 us
    psum x1 -> x0, blocking collectives: 42 us -> none  [per_device(): centre = lax.psum(picked, ('blk', 'grp')) / members]
    all_gather x3 -> x0, blocking collectives: 33.1 us -> none  [the longest x2 17.2 us: joined_2(): everything = jax.tree.map(lambda part: lax.all_gather(part, axis), shard)]
    ppermute x0 -> x13, starting transfers between devices: none -> 17.8 us  [over(): return lax.ppermute(value, axis, [(i, i ^ k) for i in range(size)])]
    pallas_call x0 -> x3, Pallas kernels: none -> 11.5 us  [the longest x1 7.71 us: per_device(): pl.pallas_call(functools.partial(score_kernel, blocks=blocks, groups=grou...]
    ppermute x0 -> x13, waiting for transfers between devices: none -> 7.92 us  [over(): return lax.ppermute(value, axis, [(i, i ^ k) for i in range(size)])]
    dot_general x3 -> x0, matrix products: 6.7 us -> none  [the longest x1 5.35 us: compute(): jnp.einsum('qd,kd->qk', queries, key_rows, precision=lax.Precision.HIGHEST)]
    all_to_all x1 -> x0, waiting for transfers between devices: 5.79 us -> none  [per_device(): lax.all_to_all(split_view, 'grp', split_axis=2, concat_axis=2, tiled=True)]
    reduce_sum x8 -> x0, other arithmetic: 3.89 us -> none  [the longest x1 1.43 us: compute(): key_norm = jnp.sum(key_rows * key_rows, -1)]
  transfers between devices with their start and end apart: 2 -> 13, of which waited for: 1 -> 4; matrix products, arithmetic and copies ran while one was open for 3% -> 2% of each run, Pallas kernels for 0% -> 5%
where the time goes in v1:
time: 41.1 us; the launch traced here: 40.9 us
  starting transfers between devices  17.8 us (43%)
  Pallas kernels  11.5 us (28%)
  waiting for transfers between devices  7.92 us (19%)
  local copies, waits for them, and re-layouts  2.83 us (7%)
  other arithmetic  0.7 us (2%)
    ppermute x13, starting transfers between devices, over(): return lax.ppermute(value, axis, [(i, i ^ k) for i in range(size)])  17.8 us
    ppermute x13, waiting for transfers between devices, over(): return lax.ppermute(value, axis, [(i, i ^ k) for i in range(size)])  7.92 us
    pallas_call x1, Pallas kernels, per_device(): pl.pallas_call(functools.partial(score_kernel, blocks=blocks, groups=grou...  7.71 us
    unnamed x30, local copies, waits for them, and re-layouts  2.74 us
    pallas_call x1, Pallas kernels, per_device(): pl.pallas_call(functools.partial(finish_kernel, groups=groups, subs=subs,...  1.97 us
    pallas_call x1, Pallas kernels, per_device(): pl.pallas_call(functools.partial(prepare_kernel, subs=subs, rows=rows, ro...  1.86 us
  transfers between devices with their start and end apart: 13, of which 4 were waited for; matrix products, arithmetic and copies ran while one was open for 2% of the time, Pallas kernels for 5%

profile of v1, /device:TPU:0, one launch (start us, length us, event | category | flops | bytes accessed | tf_op | source)
XLA Modules:
  0.0 40.9 jit_solution(2420189303313334832)
XLA Ops:
  0.0 5.1 %collective-permute-start.9 = (f32[128,256]{1,0:T(8,128)}, f32[128,256]{1,0:T(8,128)S(1)}, u32[]{:S(2)}, u32[]{:S(2)}) collective-permute-start(f32[128,256]{1,0:T(8,128)} %bitcast.2), channel_id=1, source_target_pairs={{0,3},{1,2},{2,1},{3,0},{4,7},{5,6},{6,5},{7,4},{8,11},{9,10},{10,... | collective-permute-start | bytes 393224 | tf_op jit(solution)/shard_map/ppermute | solution.py:150
  5.1 1.9 %prepare.1.refs_0_ = f32[136,256]{1,0:T(8,128)} custom-call(s32[1]{0:T(128)} %bitcast.group_ref, s32[2,4]{1,0:T(2,128)} %assign_ref.1, f32[128,256]{1,0:T(8,128)} %bitcast.4), custom_call_target="tpu_custom_call" | custom-call | tf_op jit(solution)/shard_map/prepare/pallas_call | solution.py:156
  6.9 2.4 %collective-permute-start.5 = (f32[136,256]{1,0:T(8,128)}, f32[136,256]{1,0:T(8,128)S(1)}, u32[]{:S(2)}, u32[]{:S(2)}) collective-permute-start(f32[136,256]{1,0:T(8,128)} %prepare.1.refs_0_), channel_id=1, source_target_pairs={{0,24},{4,28},{8,16},{12,20},{16,8},{20,12},{24,0},{28,4},{1,25},{... | collective-permute-start | bytes 417800 | tf_op jit(solution)/shard_map/ppermute | solution.py:150
  9.4 0.5 %collective-permute-start.3 = (f32[136,256]{1,0:T(8,128)}, f32[136,256]{1,0:T(8,128)S(1)}, u32[]{:S(2)}, u32[]{:S(2)}) collective-permute-start(f32[136,256]{1,0:T(8,128)} %prepare.1.refs_0_), channel_id=1, source_target_pairs={{0,16},{4,20},{8,24},{12,28},{16,0},{20,4},{24,8},{28,12},{1,17},{... | collective-permute-start | bytes 417800 | tf_op jit(solution)/shard_map/ppermute | solution.py:150
  9.9 0.5 %collective-permute-start.1 = (f32[136,256]{1,0:T(8,128)}, f32[136,256]{1,0:T(8,128)S(1)}, u32[]{:S(2)}, u32[]{:S(2)}) collective-permute-start(f32[136,256]{1,0:T(8,128)} %prepare.1.refs_0_), channel_id=1, source_target_pairs={{0,8},{4,12},{8,0},{12,4},{16,24},{20,28},{24,16},{28,20},{1,9},{5... | collective-permute-start | bytes 417800 | tf_op jit(solution)/shard_map/ppermute | solution.py:150
  10.4 0.7 %copy-done.14 = s32[4,16]{1,0:T(4,128)S(1)} copy-done((s32[4,16]{1,0:T(4,128)S(1)}, s32[4,16]{1,0:T(4,128)}, u32[]{:S(2)}) %copy-start.14) | copy-done | bytes 280
  11.1 0.1 eq.17
  11.2 3.8 %collective-permute-start.7 = (f32[128,256]{1,0:T(8,128)S(1)}, f32[128,256]{1,0:T(8,128)S(1)}, u32[]{:S(2)}, u32[]{:S(2)}) collective-permute-start(f32[128,256]{1,0:T(8,128)S(1)} %bitcast.5), channel_id=1, source_target_pairs={{0,1},{1,0},{2,3},{3,2},{4,5},{5,4},{6,7},{7,6},{8,9},{9,8},{10,11... | collective-permute-start | bytes 393224 | tf_op jit(solution)/shard_map/ppermute | solution.py:150
  15.1 1.4 %collective-permute-done.8.refs_9_ = f32[128,256]{1,0:T(8,128)S(1)} collective-permute-done((f32[128,256]{1,0:T(8,128)}, f32[128,256]{1,0:T(8,128)S(1)}, u32[]{:S(2)}, u32[]{:S(2)}) %collective-permute-start.8) | collective-permute-done | bytes 131104 | tf_op jit(solution)/shard_map/ppermute | solution.py:150
  16.5 0.5 %collective-permute-start.6 = (f32[136,256]{1,0:T(8,128)S(1)}, f32[136,256]{1,0:T(8,128)S(1)}, u32[]{:S(2)}, u32[]{:S(2)}) collective-permute-start(f32[136,256]{1,0:T(8,128)S(1)} %collective-permute-done.5.refs_6_), channel_id=1, source_target_pairs={{0,4},{4,0},{8,12},{12,8},{16,20},{20,16},{24,28},{28,24},{1,5},{5... | collective-permute-start | bytes 417800 | tf_op jit(solution)/shard_map/ppermute | solution.py:150
  17.0 0.1 collective-permute-start.4
  17.1 0.4 %collective-permute-start.2 = (f32[136,256]{1,0:T(8,128)S(1)}, f32[136,256]{1,0:T(8,128)S(1)}, u32[]{:S(2)}, u32[]{:S(2)}) collective-permute-start(f32[136,256]{1,0:T(8,128)S(1)} %collective-permute-done.1.refs_2_), channel_id=1, source_target_pairs={{0,4},{4,0},{8,12},{12,8},{16,20},{20,16},{24,28},{28,24},{1,5},{5... | collective-permute-start | bytes 417800 | tf_op jit(solution)/shard_map/ppermute | solution.py:150
  17.5 0.7 %fusion.hot_ref = f32[64,32]{1,0:T(8,128)} fusion(s32[64]{0:T(128)S(1)} %eq.17), kind=kLoop, calls=%fused_computation.1 | loop fusion | flops 4096 | bytes 8448 | tf_op jit(solution)/shard_map/convert_element_type | solution.py:171
  18.2 0.8 %collective-permute-done.7.refs_8_ = f32[128,256]{1,0:T(8,128)S(1)} collective-permute-done((f32[128,256]{1,0:T(8,128)S(1)}, f32[128,256]{1,0:T(8,128)S(1)}, u32[]{:S(2)}, u32[]{:S(2)}) %collective-permute-start.7) | collective-permute-done | bytes 131104 | tf_op jit(solution)/shard_map/ppermute | solution.py:150
  19.1 0.5 %copy-done.10 = f32[128,256]{1,0:T(8,128)} copy-done((f32[128,256]{1,0:T(8,128)}, f32[128,256]{1,0:T(8,128)S(1)}, u32[]{:S(2)}) %copy-start.10) | copy-done | bytes 131096
  19.8 0.7 %copy-done.6 = f32[136,256]{1,0:T(8,128)} copy-done((f32[136,256]{1,0:T(8,128)}, f32[136,256]{1,0:T(8,128)S(1)}, u32[]{:S(2)}) %copy-start.6) | copy-done | bytes 139288
  20.5 7.7 %score.1 = (f32[152,128]{1,0:T(8,128)}, f32[4,128]{1,0:T(4,128)}) custom-call(s32[2]{0:T(128)} %band_ref.3, f32[64,32]{1,0:T(8,128)} %fusion.hot_ref, f32[136,256]{1,0:T(8,128)} %prepare.1.refs_0_, f32[136,256]{1,0:T(8,128)} %copy-done.3, f32[136,256]{1,0:T(8,128)} %copy-done.2, f32[136,256]{1,0:T(8,128)} %copy-done.6, f32[136,256]{1,0:T(8,128)} %copy-done.1, ...), custom_call_target="tpu_custom_call" | custom-call | tf_op jit(solution)/shard_map/score/pallas_call | solution.py:173
  28.2 1.8 %collective-permute-start.12 = (f32[152,128]{1,0:T(8,128)}, f32[152,128]{1,0:T(8,128)S(1)}, u32[]{:S(2)}, u32[]{:S(2)}) collective-permute-start(f32[152,128]{1,0:T(8,128)} %get-tuple-element.8.refs_0_), channel_id=1, source_target_pairs={{0,3},{1,2},{2,1},{3,0},{4,7},{5,6},{6,5},{7,4},{8,11},{9,10},{10,... | collective-permute-start | bytes 233480 | tf_op jit(solution)/shard_map/ppermute | solution.py:150
  29.9 0.7 %collective-permute-start.11 = (f32[152,128]{1,0:T(8,128)}, f32[152,128]{1,0:T(8,128)S(1)}, u32[]{:S(2)}, u32[]{:S(2)}) collective-permute-start(f32[152,128]{1,0:T(8,128)} %get-tuple-element.8.refs_0_), channel_id=1, source_target_pairs={{0,2},{1,3},{2,0},{3,1},{4,6},{5,7},{6,4},{7,5},{8,10},{9,11},{10,... | collective-permute-start | bytes 233480 | tf_op jit(solution)/shard_map/ppermute | solution.py:150
  30.7 1.9 %collective-permute-start.10 = (f32[152,128]{1,0:T(8,128)}, f32[152,128]{1,0:T(8,128)S(1)}, u32[]{:S(2)}, u32[]{:S(2)}) collective-permute-start(f32[152,128]{1,0:T(8,128)} %get-tuple-element.8.refs_0_), channel_id=1, source_target_pairs={{0,1},{1,0},{2,3},{3,2},{4,5},{5,4},{6,7},{7,6},{8,9},{9,8},{10,11... | collective-permute-start | bytes 233480 | tf_op jit(solution)/shard_map/ppermute | solution.py:150
  32.6 2.8 %collective-permute-done.12.refs_3_ = f32[152,128]{1,0:T(8,128)S(1)} collective-permute-done((f32[152,128]{1,0:T(8,128)}, f32[152,128]{1,0:T(8,128)S(1)}, u32[]{:S(2)}, u32[]{:S(2)}) %collective-permute-start.12) | collective-permute-done | bytes 77856 | tf_op jit(solution)/shard_map/ppermute | solution.py:150
  35.4 2.9 %collective-permute-done.11.refs_2_ = f32[152,128]{1,0:T(8,128)S(1)} collective-permute-done((f32[152,128]{1,0:T(8,128)}, f32[152,128]{1,0:T(8,128)S(1)}, u32[]{:S(2)}, u32[]{:S(2)}) %collective-permute-start.11) | collective-permute-done | bytes 77856 | tf_op jit(solution)/shard_map/ppermute | solution.py:150
  38.3 0.6 %copy-done.12 = f32[152,128]{1,0:T(8,128)} copy-done((f32[152,128]{1,0:T(8,128)}, f32[152,128]{1,0:T(8,128)S(1)}, u32[]{:S(2)}) %copy-start.12) | copy-done | bytes 77848
  38.9 2.0 %finish.1 = f32[2,4,32]{2,1,0:T(4,128)} custom-call(s32[2]{0:T(128)} %band_ref.3, f32[4,128]{1,0:T(4,128)} %get-tuple-element.7.norm_ref, f32[152,128]{1,0:T(8,128)} %get-tuple-element.8.refs_0_, f32[152,128]{1,0:T(8,128)} %copy-done.13, f32[152,128]{1,0:T(8,128)} %copy-done.12, f32[152,128]{1,0:T(8,128)} %copy-done.11), custom_call_target="tpu_custom_call" | custom-call | tf_op jit(solution)/shard_map/finish/pallas_call | solution.py:198
  (38 shorter events, 0.3 us)
Async XLA Ops:
  0.0 11.2 %collective-permute-start.9 = (f32[128,256]{1,0:T(8,128)}, f32[128,256]{1,0:T(8,128)S(1)}, u32[]{:S(2)}, u32[]{:S(2)}) collective-permute-start(f32[128,256]{1,0:T(8,128)} %bitcast.2), channel_id=1, source_target_pairs={{0,3},{1,2},{2,1},{3,0},{4,7},{5,6},{6,5},{7,4},{8,11},{9,10},{10,... | collective-permute-start | bytes 393224 | tf_op jit(solution)/shard_map/ppermute | solution.py:150
  5.1 11.4 %collective-permute-start.8 = (f32[128,256]{1,0:T(8,128)}, f32[128,256]{1,0:T(8,128)S(1)}, u32[]{:S(2)}, u32[]{:S(2)}) collective-permute-start(f32[128,256]{1,0:T(8,128)} %bitcast.3), channel_id=1, source_target_pairs={{0,2},{1,3},{2,0},{3,1},{4,6},{5,7},{6,4},{7,5},{8,10},{9,11},{10,... | collective-permute-start | bytes 393224 | tf_op jit(solution)/shard_map/ppermute | solution.py:150
  5.1 6.1 %copy-start.7 = (f32[4,32,256]{2,1,0:T(8,128)S(1)}, f32[4,32,256]{2,1,0:T(8,128)}, u32[]{:S(2)}) copy-start(f32[4,32,256]{2,1,0:T(8,128)} %param.4) | copy-start | bytes 393220
  6.9 9.5 %collective-permute-start.5 = (f32[136,256]{1,0:T(8,128)}, f32[136,256]{1,0:T(8,128)S(1)}, u32[]{:S(2)}, u32[]{:S(2)}) collective-permute-start(f32[136,256]{1,0:T(8,128)} %prepare.1.refs_0_), channel_id=1, source_target_pairs={{0,24},{4,28},{8,16},{12,20},{16,8},{20,12},{24,0},{28,4},{1,25},{... | collective-permute-start | bytes 417800 | tf_op jit(solution)/shard_map/ppermute | solution.py:150
  9.4 7.6 %collective-permute-start.3 = (f32[136,256]{1,0:T(8,128)}, f32[136,256]{1,0:T(8,128)S(1)}, u32[]{:S(2)}, u32[]{:S(2)}) collective-permute-start(f32[136,256]{1,0:T(8,128)} %prepare.1.refs_0_), channel_id=1, source_target_pairs={{0,16},{4,20},{8,24},{12,28},{16,0},{20,4},{24,8},{28,12},{1,17},{... | collective-permute-start | bytes 417800 | tf_op jit(solution)/shard_map/ppermute | solution.py:150
  9.9 7.2 %collective-permute-start.1 = (f32[136,256]{1,0:T(8,128)}, f32[136,256]{1,0:T(8,128)S(1)}, u32[]{:S(2)}, u32[]{:S(2)}) collective-permute-start(f32[136,256]{1,0:T(8,128)} %prepare.1.refs_0_), channel_id=1, source_target_pairs={{0,8},{4,12},{8,0},{12,4},{16,24},{20,28},{24,16},{28,20},{1,9},{5... | collective-permute-start | bytes 417800 | tf_op jit(solution)/shard_map/ppermute | solution.py:150
  10.4 0.7 %copy-start.14 = (s32[4,16]{1,0:T(4,128)S(1)}, s32[4,16]{1,0:T(4,128)}, u32[]{:S(2)}) copy-start(s32[4,16]{1,0:T(4,128)} %param.5) | copy-start | bytes 772
  11.2 7.8 %copy-start.8 = (f32[128,256]{1,0:T(8,128)}, f32[128,256]{1,0:T(8,128)S(1)}, u32[]{:S(2)}) copy-start(f32[128,256]{1,0:T(8,128)S(1)} %collective-permute-done.9.refs_10_) | copy-start | bytes 393220
  11.2 7.8 %collective-permute-start.7 = (f32[128,256]{1,0:T(8,128)S(1)}, f32[128,256]{1,0:T(8,128)S(1)}, u32[]{:S(2)}, u32[]{:S(2)}) collective-permute-start(f32[128,256]{1,0:T(8,128)S(1)} %bitcast.5), channel_id=1, source_target_pairs={{0,1},{1,0},{2,3},{3,2},{4,5},{5,4},{6,7},{7,6},{8,9},{9,8},{10,11... | collective-permute-start | bytes 393224 | tf_op jit(solution)/shard_map/ppermute | solution.py:150
  16.5 2.6 %copy-start.9 = (f32[128,256]{1,0:T(8,128)}, f32[128,256]{1,0:T(8,128)S(1)}, u32[]{:S(2)}) copy-start(f32[128,256]{1,0:T(8,128)S(1)} %collective-permute-done.8.refs_9_) | copy-start | bytes 393220
  16.5 2.5 %collective-permute-start = (f32[136,256]{1,0:T(8,128)}, f32[136,256]{1,0:T(8,128)S(1)}, u32[]{:S(2)}, u32[]{:S(2)}) collective-permute-start(f32[136,256]{1,0:T(8,128)} %prepare.1.refs_0_), channel_id=1, source_target_pairs={{0,4},{4,0},{8,12},{12,8},{16,20},{20,16},{24,28},{28,24},{1,5},{5... | collective-permute-start | bytes 417800 | tf_op jit(solution)/shard_map/ppermute | solution.py:150
  16.5 2.6 %copy-start = (f32[136,256]{1,0:T(8,128)}, f32[136,256]{1,0:T(8,128)S(1)}, u32[]{:S(2)}) copy-start(f32[136,256]{1,0:T(8,128)S(1)} %collective-permute-done.5.refs_6_) | copy-start | bytes 417796
  16.5 2.5 %collective-permute-start.6 = (f32[136,256]{1,0:T(8,128)S(1)}, f32[136,256]{1,0:T(8,128)S(1)}, u32[]{:S(2)}, u32[]{:S(2)}) collective-permute-start(f32[136,256]{1,0:T(8,128)S(1)} %collective-permute-done.5.refs_6_), channel_id=1, source_target_pairs={{0,4},{4,0},{8,12},{12,8},{16,20},{20,16},{24,28},{28,24},{1,5},{5... | collective-permute-start | bytes 417800 | tf_op jit(solution)/shard_map/ppermute | solution.py:150
  17.0 2.1 %copy-start.1 = (f32[136,256]{1,0:T(8,128)}, f32[136,256]{1,0:T(8,128)S(1)}, u32[]{:S(2)}) copy-start(f32[136,256]{1,0:T(8,128)S(1)} %collective-permute-done.3.refs_4_) | copy-start | bytes 417796
  17.0 2.0 %collective-permute-start.4 = (f32[136,256]{1,0:T(8,128)S(1)}, f32[136,256]{1,0:T(8,128)S(1)}, u32[]{:S(2)}, u32[]{:S(2)}) collective-permute-start(f32[136,256]{1,0:T(8,128)S(1)} %collective-permute-done.3.refs_4_), channel_id=1, source_target_pairs={{0,4},{4,0},{8,12},{12,8},{16,20},{20,16},{24,28},{28,24},{1,5},{5... | collective-permute-start | bytes 417800 | tf_op jit(solution)/shard_map/ppermute | solution.py:150
  17.1 2.0 %copy-start.2 = (f32[136,256]{1,0:T(8,128)}, f32[136,256]{1,0:T(8,128)S(1)}, u32[]{:S(2)}) copy-start(f32[136,256]{1,0:T(8,128)S(1)} %collective-permute-done.1.refs_2_) | copy-start | bytes 417796
  17.1 2.0 %collective-permute-start.2 = (f32[136,256]{1,0:T(8,128)S(1)}, f32[136,256]{1,0:T(8,128)S(1)}, u32[]{:S(2)}, u32[]{:S(2)}) collective-permute-start(f32[136,256]{1,0:T(8,128)S(1)} %collective-permute-done.1.refs_2_), channel_id=1, source_target_pairs={{0,4},{4,0},{8,12},{12,8},{16,20},{20,16},{24,28},{28,24},{1,5},{5... | collective-permute-start | bytes 417800 | tf_op jit(solution)/shard_map/ppermute | solution.py:150
  19.0 0.7 %copy-start.3 = (f32[136,256]{1,0:T(8,128)}, f32[136,256]{1,0:T(8,128)S(1)}, u32[]{:S(2)}) copy-start(f32[136,256]{1,0:T(8,128)S(1)} %collective-permute-done.refs_1_) | copy-start | bytes 417796
  19.0 0.8 %copy-start.4 = (f32[136,256]{1,0:T(8,128)}, f32[136,256]{1,0:T(8,128)S(1)}, u32[]{:S(2)}) copy-start(f32[136,256]{1,0:T(8,128)S(1)} %collective-permute-done.6.refs_7_) | copy-start | bytes 417796
  19.0 0.8 %copy-start.5 = (f32[136,256]{1,0:T(8,128)}, f32[136,256]{1,0:T(8,128)S(1)}, u32[]{:S(2)}) copy-start(f32[136,256]{1,0:T(8,128)S(1)} %collective-permute-done.4.refs_5_) | copy-start | bytes 417796
  28.2 7.2 %collective-permute-start.12 = (f32[152,128]{1,0:T(8,128)}, f32[152,128]{1,0:T(8,128)S(1)}, u32[]{:S(2)}, u32[]{:S(2)}) collective-permute-start(f32[152,128]{1,0:T(8,128)} %get-tuple-element.8.refs_0_), channel_id=1, source_target_pairs={{0,3},{1,2},{2,1},{3,0},{4,7},{5,6},{6,5},{7,4},{8,11},{9,10},{10,... | collective-permute-start | bytes 233480 | tf_op jit(solution)/shard_map/ppermute | solution.py:150
  29.9 8.3 %collective-permute-start.11 = (f32[152,128]{1,0:T(8,128)}, f32[152,128]{1,0:T(8,128)S(1)}, u32[]{:S(2)}, u32[]{:S(2)}) collective-permute-start(f32[152,128]{1,0:T(8,128)} %get-tuple-element.8.refs_0_), channel_id=1, source_target_pairs={{0,2},{1,3},{2,0},{3,1},{4,6},{5,7},{6,4},{7,5},{8,10},{9,11},{10,... | collective-permute-start | bytes 233480 | tf_op jit(solution)/shard_map/ppermute | solution.py:150
  30.7 7.6 %collective-permute-start.10 = (f32[152,128]{1,0:T(8,128)}, f32[152,128]{1,0:T(8,128)S(1)}, u32[]{:S(2)}, u32[]{:S(2)}) collective-permute-start(f32[152,128]{1,0:T(8,128)} %get-tuple-element.8.refs_0_), channel_id=1, source_target_pairs={{0,1},{1,0},{2,3},{3,2},{4,5},{5,4},{6,7},{7,6},{8,9},{9,8},{10,11... | collective-permute-start | bytes 233480 | tf_op jit(solution)/shard_map/ppermute | solution.py:150
  35.3 2.9 %copy-start.11 = (f32[152,128]{1,0:T(8,128)}, f32[152,128]{1,0:T(8,128)S(1)}, u32[]{:S(2)}) copy-start(f32[152,128]{1,0:T(8,128)S(1)} %collective-permute-done.12.refs_3_) | copy-start | bytes 233476
  (4 other events, 2.6 us)
